TPU v7x, 32 devices: a whole 2x2x4 slice. The times are simulated.
32 devices in a mesh: dp: 4 (over y, x), mp: 8 (over z, core).
Axes of the slice: x: 2, y: 2, z: 4, core: 2. Of those that a mesh axis runs over, the one named last changes fastest.
Arguments:
- stored: float32 [16384, 18432], P(('dp', 'mp')), may hold values from -0.046875 to 0.046875
- row_map: int32 [16384], replicated, may hold values from 0 to 16383, as said below
- probe: bfloat16 [16384, 1024], P('dp'), may hold values from -6 to 6
- lane: bfloat16 [128, 1024], replicated, may hold values from -6 to 6
Outputs:
- shards: bfloat16 [144, 128, 16384], P('mp', None, 'dp')
- slab_checks: float32 [144, 32, 1024], P('mp', 'dp')
- head_sums: float32 [144, 1024], P('mp')
Inputs may be any that keep to these rules, and one draw needn't show every extreme that they name: row_map is a permutation of 0..16383 with row_map[i] // 4096 == (i % 512) // 128 for every stored row i.
All inputs are finite; a program needn't handle non-finite values.
Results may differ from a plain program's by a relative error of at most 0.0029.
Values may be sent and summed in bfloat16 or wider, within the bound.
A program may use at most 128 MiB of HBM per device.

v0:
```python
import jax
import jax.numpy as jnp
from jax import lax
from jax.sharding import PartitionSpec as P

Q_HEADS = 128
KV_HEADS = 8
HD = 128
PROBES = 1024
SLABS = 8


def body(stored, row_map, probe, lane):
    n_dp = lax.axis_size("dp")
    n_mp = lax.axis_size("mp")
    rows_dev = stored.shape[0]
    sub_rows = rows_dev // n_dp
    per_device = Q_HEADS // n_mp
    slot_count = per_device + 2
    kv_share = n_mp // KV_HEADS
    narrow = stored.astype(jnp.bfloat16)
    query_cols = narrow[:, : Q_HEADS * HD].reshape(rows_dev, n_mp, per_device * HD)
    key_block = narrow[:, Q_HEADS * HD : (Q_HEADS + KV_HEADS) * HD].reshape(
        rows_dev, KV_HEADS, 1, HD
    )
    value_block = narrow[:, (Q_HEADS + KV_HEADS) * HD :].reshape(rows_dev, KV_HEADS, 1, HD)
    key_cols = key_block.reshape(rows_dev, n_mp, HD)
    value_cols = value_block.reshape(rows_dev, n_mp, HD)
    outgoing = jnp.concatenate([query_cols, key_cols, value_cols], axis=2)
    outgoing = outgoing.reshape(n_dp, sub_rows, n_mp, slot_count * HD)
    by_heads = lax.all_to_all(outgoing, "mp", split_axis=2, concat_axis=2, tiled=True)
    incoming = lax.all_to_all(by_heads, "dp", split_axis=0, concat_axis=0, tiled=True)
    arrived = jnp.transpose(incoming, (0, 2, 1, 3)).reshape(n_dp * n_mp * sub_rows, slot_count * HD)
    group_rows = arrived.shape[0]
    my_group = lax.axis_index("dp")
    stored_index = (
        jnp.arange(n_dp * n_mp, dtype=jnp.int32)[:, None] * rows_dev
        + my_group * sub_rows
        + jnp.arange(sub_rows, dtype=jnp.int32)[None, :]
    )
    local_row = jnp.take(row_map, stored_index.reshape(-1)) - my_group * group_rows
    inverse = (
        jnp.zeros((group_rows,), jnp.int32)
        .at[local_row]
        .set(jnp.arange(group_rows, dtype=jnp.int32))
    )
    placed = jnp.take(arrived, inverse, axis=0)
    shards = jnp.transpose(placed.reshape(group_rows, slot_count, HD), (1, 2, 0))
    slab_rows = group_rows // SLABS
    lane_wide = lane.astype(jnp.float32)
    slab_list = []
    running = jnp.zeros((slot_count, PROBES), jnp.float32)
    for slab_index in range(SLABS):
        slab_block = shards[:, :, slab_index * slab_rows : (slab_index + 1) * slab_rows]
        probe_rows = probe[slab_index * slab_rows : (slab_index + 1) * slab_rows]
        projected = jnp.einsum(
            "jer,rp->jep", slab_block, probe_rows, preferred_element_type=jnp.float32
        )
        slab_sum = jnp.sum(projected * lane_wide[None], axis=1)
        slab_list.append(slab_sum)
        running = running + lax.psum(slab_sum, "dp")
    slab_checks = jnp.stack(slab_list, axis=1)
    head_sums = running / (n_dp * SLABS)
    return (shards, slab_checks, head_sums)


def solution(mesh):
    return jax.shard_map(
        body,
        mesh=mesh,
        in_specs=(P(("dp", "mp"), None), P(), P("dp", None), P()),
        out_specs=(P("mp", None, "dp"), P("mp", "dp", None), P("mp", None)),
        check_vma=False,
    )
```

profile of v0, /device:TPU:0, one launch (start us, length us, event | category | flops | bytes accessed | tf_op | source)
XLA Modules:
  0.0 843.1 jit_solution(1945808742808194949)
XLA Ops:
  7.2 13.5 %convert_element_type.6 = bf16[512,18432]{1,0:T(8,128)(2,1)S(1)} convert(f32[512,18432]{1,0:T(8,128)} %param.4) | non-fusion elementwise | flops 9437184 | bytes 56623104 | tf_op jit(solution)/shard_map/convert_element_type | solution.py:21
  20.7 0.2 slice_bitcast_fusion.1
  20.9 1.2 slice.80
  22.1 0.3 copy.30
  22.4 0.3 copy.29
  22.7 10.4 %copy.28 = bf16[64,8,8,2048]{3,2,1,0:T(8,128)(2,1)S(1)} copy(bf16[64,8,8,2048]{3,1,2,0:T(8,128)(2,1)S(1)} %bitcast.62) | data formatting | bytes 33554432
  33.1 12.2 %pad_maximum_fusion = bf16[4,128,8,2304]{3,2,1,0:T(8,128)(2,1)S(1)} fusion(bf16[4,128,8,128]{3,2,1,0:T(8,128)(2,1)S(1)} %bitcast.64, bf16[4,128,8,128]{3,2,1,0:T(8,128)(2,1)S(1)} %bitcast.65, bf16[4,128,8,2048]{3,2,1,0:T(8,128)(2,1)S(1)} %bitcast.63), kind=kLoop, calls=%fused_computation.3 | loop fusion | flops 56623104 | bytes 37748736 | tf_op jit(solution)/shard_map/concatenate | solution.py:29
  45.4 8.7 %copy.24 = bf16[4,128,8,2304]{3,1,0,2:T(8,128)(2,1)S(1)} copy(bf16[4,128,8,2304]{3,2,1,0:T(8,128)(2,1)S(1)} %pad_maximum_fusion) | data formatting | bytes 37748736 | tf_op jit(solution)/shard_map/concatenate | solution.py:29
  54.1 414.7 %all_to_all.10 = bf16[4,128,8,2304]{3,1,0,2:T(8,128)(2,1)S(1)} all-to-all(bf16[4,128,8,2304]{3,1,0,2:T(8,128)(2,1)S(1)} %copy.24), channel_id=1, replica_groups=mesh['dp'=4,'mp'=8] {'mp'}, dimensions={2} | all-to-all | bytes 37748736 | tf_op jit(solution)/shard_map/all_to_all | solution.py:31
  468.8 6.6 copy.25
  475.5 7.5 all-to-all-start.1
  483.1 0.1 iota_add_fusion
  483.2 23.0 %gather_fusion = s32[4096]{0:T(1024)S(1)} fusion(s32[16384]{0:T(1024)S(1)} %copy-done, s32[4096]{0:T(1024)S(1)} %broadcast_clamp_fusion), kind=kCustom, calls=%fused_computation | custom fusion | bytes 49152 | tf_op jit(solution)/shard_map/jit(_take)/gather | solution.py:41
  506.2 0.1 compare_select_fusion
  506.3 15.5 %scatter_custom_fusion = s32[4096]{0:T(1024)S(1)} fusion(s32[4096]{0:T(1024)S(1)} %bitcast.70, s32[4096]{0:T(1024)S(1)} %iota.13, s32[]{:T(128)} %constant.21.clone.1), kind=kCustom, calls=%fused_computation.57 | custom fusion | bytes 16388 | tf_op jit(solution)/shard_map/scatter | solution.py:45
  521.9 165.7 %all-to-all-done.1 = bf16[4,128,8,2304]{3,1,2,0:T(8,128)(2,1)} async-done(((bf16[4,128,8,2304]{3,1,2,0:T(8,128)(2,1)}), bf16[4,128,8,2304]{3,1,2,0:T(8,128)(2,1)}, u32[]{:S(2)}, u32[]{:S(2)}) %all-to-all-start.1) | async-done | bytes 18874400 | tf_op jit(solution)/shard_map/all_to_all | solution.py:32
  687.5 44.1 %gather_fusion.1 = bf16[4096,2304]{1,0:T(8,128)(2,1)} fusion(bf16[4096,2304]{1,0:T(8,128)(2,1)} %bitcast.5, s32[4096]{0:T(1024)S(1)} %fusion.24), kind=kCustom, calls=%fused_computation.1 | custom fusion | bytes 37765120 | tf_op jit(solution)/shard_map/jit(_take)/gather | solution.py:47
  731.6 23.6 %copy.26 = bf16[4096,2304]{0,1:T(8,128)(2,1)} copy(bf16[4096,2304]{1,0:T(8,128)(2,1)} %gather_fusion.1) | data formatting | bytes 37748736 | tf_op jit(solution)/shard_map/jit(_take)/gather | solution.py:47
  755.3 9.5 %select_bitcast_fusion = bf16[18,128,4096]{2,1,0:T(8,128)(2,1)S(1)} fusion(bf16[4096,18,128]{0,2,1:T(8,128)(2,1)} %bitcast.61, pred[4096]{0:T(1024)(128)(4,1)S(1)} %compare_and_fusion), kind=kLoop, calls=%fused_computation.4 | loop fusion | flops 9437184 | bytes 37752832 | tf_op jit(solution)/shard_map/transpose | solution.py:48
  764.8 5.0 multiply_reduce_fusion.7
  769.8 5.5 multiply_reduce_fusion.6
  775.3 0.6 slice-done.1
  775.9 2.8 multiply_reduce_fusion.5
  778.7 2.9 multiply_reduce_fusion.4
  781.6 2.8 multiply_reduce_fusion.3
  784.4 2.9 multiply_reduce_fusion.2
  787.3 2.8 multiply_reduce_fusion.1
  790.2 2.9 multiply_reduce_fusion
  793.2 0.7 add_add_fusion
  793.9 1.2 copy.27
  795.1 39.6 %all-reduce.2.cloned.1.call-done = f32[18,1024]{1,0:T(8,128)} async-done(((f32[18,1024]{1,0:T(8,128)}), f32[18,1024]{1,0:T(8,128)}) %all-reduce.2.cloned.1.call-update) | async-done | bytes 73744 | tf_op jit(solution)/shard_map/psum | solution.py:61
  834.7 1.5 broadcast_multiply_fusion
  (29 shorter events, 0.3 us)
Async XLA Ops:
  7.2 476.0 %copy-start = (s32[16384]{0:T(1024)S(1)}, s32[16384]{0:T(1024)}, u32[]{:S(2)}) copy-start(s32[16384]{0:T(1024)} %param.5) | copy-start | bytes 196612
  475.5 7.5 copy-start.3
  475.5 212.1 %all-to-all-start.1 = ((bf16[4,128,8,2304]{3,1,2,0:T(8,128)(2,1)}), bf16[4,128,8,2304]{3,1,2,0:T(8,128)(2,1)}, u32[]{:S(2)}, u32[]{:S(2)}) async-start(bf16[4,128,8,2304]{3,1,2,0:T(8,128)(2,1)} %copy.25), calls=%async_computation.1 | async-start | bytes 37748736 | tf_op jit(solution)/shard_map/all_to_all | solution.py:32
  482.9 351.7 %all-reduce.2.cloned.1.call-start = ((), (), s32[]{:S(2)}) async-start(), calls=%async_computation.2 | async-start | bytes 196608 | tf_op jit(solution)/shard_map/psum | solution.py:61
  764.8 25.4 %copy-start.2 = (bf16[18,128,4096]{2,1,0:T(8,128)(2,1)}, bf16[18,128,4096]{2,1,0:T(8,128)(2,1)S(1)}, u32[]{:S(2)}) copy-start(bf16[18,128,4096]{2,1,0:T(8,128)(2,1)S(1)} %select_bitcast_fusion) | copy-start | bytes 56623108
  764.8 10.5 %slice-start = ((s8[8388608]{0:T(1024)(128)(4,1)}), s8[4194304]{0:T(1024)(128)(4,1)S(1)}, s32[]{:S(2)}) async-start(s8[8388608]{0:T(1024)(128)(4,1)} %bitcast.71), calls=%async_computation.3 | async-start | bytes 8388608
  769.8 6.1 slice-start.1
  787.3 48.9 %copy-start.1 = (s32[16384]{0:T(1024)S(1)}, s32[16384]{0:T(1024)}, u32[]{:S(2)}) copy-start(s32[16384]{0:T(1024)} %param.5) | copy-start | bytes 196612
Sparse Core Ops, SparseCore 0:
  794.0 40.6 all-reduce.1
where the time goes:
time: 844 us; the launch traced here: 843 us
  blocking collectives  415 us (49%)
  waiting for transfers between devices  205 us (24%)
  local copies, waits for them, and re-layouts  136 us (16%)
  other arithmetic  37.7 us (4%)
  matrix products  27.6 us (3%)
  between operations  14.4 us (2%)
    all_to_all x1, blocking collectives, body(): lax.all_to_all(outgoing, 'mp', split_axis=2, concat_axis=2, tiled=True)  415 us
    all_to_all x1, waiting for transfers between devices, body(): lax.all_to_all(by_heads, 'dp', split_axis=0, concat_axis=0, tiled=True)  166 us
    gather x2, local copies, waits for them, and re-layouts, body(): placed = jnp.take(arrived, inverse, axis=0)  67.7 us
    psum x1, waiting for transfers between devices, body(): running = running + lax.psum(slab_sum, 'dp')  39.6 us
    dot_general x8, matrix products, body(): jnp.einsum('jer,rp->jep', slab_block, probe_rows, preferred_element_type=...  27.6 us
    gather x1, local copies, waits for them, and re-layouts, body(): jnp.take(row_map, stored_index.reshape(-1)) - my_group * group_rows  23 us
  transfers between devices with their start and end apart: 2, of which 2 were waited for; matrix products, arithmetic and copies ran while one was open for 5% of the time, Pallas kernels for 0%

commit v1 on v0

v1 whole, which is shorter than its diff:
```python
import functools

import jax
import jax.numpy as jnp
from jax import lax
from jax.experimental import pallas as pl
from jax.experimental.pallas import tpu as pltpu
from jax.sharding import PartitionSpec as P

Q_HEADS = 128
KV_HEADS = 8
HD = 128
SLABS = 8
PAIR = 2
AHEAD = 3
MESH = pl.DeviceIdType.MESH


def kernel(
    n_dp, n_mp, stored, local_row, probe, lane,
    shards, checks, heads, narrow, landing,
    onehot, wide, cast, arrived, turned, placed, slab_sums, sums,
    load_sem, local_sem, send_sem, recv_sem, out_sem, sum_send, sum_recv,
):
    my_dp = lax.axis_index("dp")
    my_mp = lax.axis_index("mp")
    n_dev = n_dp * n_mp
    me = my_dp * n_mp + my_mp
    rows_dev = stored.shape[0]
    sub = rows_dev // n_dp
    group_rows = probe.shape[0]
    slab_rows = group_rows // SLABS
    per_device = Q_HEADS // n_mp
    slots = per_device + 2
    share = n_mp // KV_HEADS
    chunks = slots // PAIR
    width = PAIR * HD

    barrier = pltpu.get_barrier_semaphore()

    def peer(k):
        return lax.rem(my_dp + k // n_mp, n_dp), lax.rem(my_mp + lax.rem(k, n_mp), n_mp)

    @pl.loop(1, n_dev)
    def _(k):
        pl.semaphore_signal(barrier, inc=1, device_id=peer(k), device_id_type=MESH)

    def load(step):
        copies = []
        for m in range(n_mp):
            if isinstance(step, int) and step == 0:
                for pos, head in enumerate((Q_HEADS + m // share, Q_HEADS + KV_HEADS + m // share)):
                    copies.append((stored.at[:, pl.ds(head * HD, HD)], wide.at[m, :, pl.ds(pos * HD, HD)]))
            else:
                first = pl.multiple_of((m * per_device + (step - 1) * PAIR) * HD, HD)
                copies.append((stored.at[:, pl.ds(first, width)], wide.at[m]))
        for src, dst in copies:
            pltpu.make_async_copy(src, dst, load_sem).start()
        pltpu.make_async_copy(wide, wide, load_sem).wait()

    def issue(step):
        load(step)

        @pl.loop(0, n_dp)
        def _(d):
            for m in range(n_mp):
                cast[d * n_mp + m] = wide[m, pl.ds(pl.multiple_of(d * sub, sub), sub), :].astype(jnp.bfloat16)

        to_narrow = pltpu.make_async_copy(cast, narrow.at[step], local_sem.at[0])
        own = pltpu.make_async_copy(cast.at[me], landing.at[step, me], local_sem.at[1])
        to_narrow.start()
        own.start()
        to_narrow.wait()
        own.wait()

        @pl.loop(1, n_dev)
        def _(k):
            dp, mp = peer(k)
            pltpu.make_async_remote_copy(
                src_ref=narrow.at[step, dp * n_mp + mp],
                dst_ref=landing.at[step, me],
                send_sem=send_sem.at[step],
                recv_sem=recv_sem.at[step],
                device_id=(dp, mp),
                device_id_type=MESH,
            ).start()

    pl.semaphore_wait(barrier, n_dev - 1)
    ahead = min(AHEAD, chunks)
    for step in range(ahead):
        issue(step)

    @pl.loop(0, SLABS)
    def _(i):
        rows = pl.ds(pl.multiple_of(i * slab_rows, slab_rows), slab_rows)
        target = local_row[rows, :]

        @pl.loop(0, SLABS)
        def _(j):
            first = pl.multiple_of(j * slab_rows, slab_rows)
            column = lax.broadcasted_iota(jnp.int32, (slab_rows, slab_rows), 1) + first
            onehot[rows, pl.ds(first, slab_rows)] = jnp.where(column == target, 1.0, 0.0).astype(jnp.bfloat16)

    group = max(1, HD // sub)
    span = group * sub

    def all_of(step):
        part = landing.at[step, pl.ds(0, n_dev - 1)]
        return pltpu.make_async_copy(part, part, recv_sem.at[step])

    def out_copy(first_slot):
        return pltpu.make_async_copy(placed, shards.at[pl.ds(first_slot, PAIR)], out_sem)

    @pl.loop(0, chunks)
    def _(step):
        first_slot = lax.rem(step * PAIR + per_device, slots)

        @pl.when(step + ahead < chunks)
        def _():
            issue(step + ahead)

        all_of(step).wait()
        fetch = pltpu.make_async_copy(landing.at[step], arrived, local_sem.at[0])
        fetch.start()
        fetch.wait()

        @pl.loop(0, n_dev // group)
        def _(b):
            rows = arrived[pl.ds(b * group, group)].astype(jnp.float32).reshape(span, width)
            turned[:, pl.ds(pl.multiple_of(b * span, span), span)] = rows.T.astype(jnp.bfloat16)

        @pl.when(step > 0)
        def _():
            out_copy(0).wait()

        @pl.loop(0, SLABS)
        def _(s):
            rows = pl.ds(pl.multiple_of(s * slab_rows, slab_rows), slab_rows)
            block = jnp.dot(turned[...], onehot[:, rows], preferred_element_type=jnp.float32).astype(jnp.bfloat16)
            placed[:, :, rows] = block.reshape(PAIR, HD, slab_rows)
            projected = jnp.dot(block, probe[rows, :], preferred_element_type=jnp.float32)
            weighted = projected.reshape(PAIR, HD, -1) * lane[...].astype(jnp.float32)[None]
            slab_sums[s] = jnp.sum(weighted, axis=1)

        out_copy(first_slot).start()
        for s in range(SLABS):
            for pos in range(PAIR):
                checks[first_slot + pos, s : s + 1, :] = slab_sums[s, pos : pos + 1, :]

    sums[my_dp] = jnp.sum(checks[...], axis=1)
    out_copy(0).wait()

    @pl.loop(1, n_dp)
    def _(k):
        pltpu.make_async_remote_copy(
            src_ref=sums.at[my_dp],
            dst_ref=sums.at[my_dp],
            send_sem=sum_send,
            recv_sem=sum_recv,
            device_id=(lax.rem(my_dp + k, n_dp), my_mp),
            device_id_type=MESH,
        ).start()

    others = sums.at[pl.ds(0, n_dp - 1)]
    pltpu.make_async_copy(others, others, sum_recv).wait()
    pltpu.make_async_copy(others, others, sum_send).wait()
    total = sums[0]
    for d in range(1, n_dp):
        total = total + sums[d]
    heads[...] = total / (n_dp * SLABS)

    @pl.loop(0, chunks)
    def _(step):
        part = narrow.at[step, pl.ds(0, n_dev - 1)]
        pltpu.make_async_copy(part, part, send_sem.at[step]).wait()


def body(stored, row_map, probe, lane):
    n_dp = lax.axis_size("dp")
    n_mp = lax.axis_size("mp")
    n_dev = n_dp * n_mp
    rows_dev, cols = stored.shape
    sub = rows_dev // n_dp
    group_rows, probes = probe.shape
    slots = Q_HEADS // n_mp + 2
    chunks = slots // PAIR
    width = PAIR * HD
    my_dp = lax.axis_index("dp")
    local_row = lax.dynamic_index_in_dim(row_map.reshape(n_dev, n_dp, sub), my_dp, 1, False)
    local_row = local_row.reshape(group_rows, 1) - my_dp * group_rows
    vmem = pl.BlockSpec(memory_space=pltpu.VMEM)
    hbm = pl.BlockSpec(memory_space=pl.ANY)
    moved = jax.ShapeDtypeStruct((chunks, n_dev, sub, width), jnp.bfloat16)
    shards, checks, heads, _, _ = pl.pallas_call(
        functools.partial(kernel, n_dp, n_mp),
        out_shape=(
            jax.ShapeDtypeStruct((slots, HD, group_rows), jnp.bfloat16),
            jax.ShapeDtypeStruct((slots, SLABS, probes), jnp.float32),
            jax.ShapeDtypeStruct((slots, probes), jnp.float32),
            moved,
            moved,
        ),
        in_specs=[hbm, vmem, vmem, vmem],
        out_specs=(hbm, vmem, vmem, hbm, hbm),
        scratch_shapes=[
            pltpu.VMEM((group_rows, group_rows), jnp.bfloat16),
            pltpu.VMEM((n_mp, rows_dev, width), jnp.float32),
            pltpu.VMEM((n_dev, sub, width), jnp.bfloat16),
            pltpu.VMEM((n_dev, sub, width), jnp.bfloat16),
            pltpu.VMEM((width, group_rows), jnp.bfloat16),
            pltpu.VMEM((PAIR, HD, group_rows), jnp.bfloat16),
            pltpu.VMEM((SLABS, PAIR, probes), jnp.float32),
            pltpu.VMEM((n_dp, slots, probes), jnp.float32),
            pltpu.SemaphoreType.DMA,
            pltpu.SemaphoreType.DMA((2,)),
            pltpu.SemaphoreType.DMA((chunks,)),
            pltpu.SemaphoreType.DMA((chunks,)),
            pltpu.SemaphoreType.DMA,
            pltpu.SemaphoreType.DMA,
            pltpu.SemaphoreType.DMA,
        ],
        compiler_params=pltpu.CompilerParams(
            collective_id=0, has_side_effects=True, vmem_limit_bytes=66_000_000
        ),
    )(stored, local_row, probe, lane)
    return shards, checks, heads


def solution(mesh):
    return jax.shard_map(
        body,
        mesh=mesh,
        in_specs=(P(("dp", "mp"), None), P(), P("dp", None), P()),
        out_specs=(P("mp", None, "dp"), P("mp", "dp", None), P("mp", None)),
        check_vma=False,
    )
```

time: 844 us -> 475 us (0.56)
  Pallas kernels: 0 us -> 451 us
  blocking collectives: 415 us -> 0 us
  waiting for transfers between devices: 205 us -> 0 us
  local copies, waits for them, and re-layouts: 136 us -> 20.3 us
  other arithmetic: 37.7 us -> 0.86 us
  matrix products: 27.6 us -> 0 us
  between operations: 14.4 us -> 0.66 us
    pallas_call x0 -> x1, Pallas kernels: none -> 451 us  [body(): pl.pallas_call(functools.partial(kernel, n_dp, n_mp), out_shape=(jax.Shap...]
    all_to_all x1 -> x0, blocking collectives: 415 us -> none  [body(): lax.all_to_all(outgoing, 'mp', split_axis=2, concat_axis=2, tiled=True)]
    all_to_all x1 -> x0, waiting for transfers between devices: 166 us -> none  [body(): lax.all_to_all(by_heads, 'dp', split_axis=0, concat_axis=0, tiled=True)]
    gather x3 -> x0, local copies, waits for them, and re-layouts: 90.7 us -> none  [the longest x2 67.7 us: body(): placed = jnp.take(arrived, inverse, axis=0)]
    psum x1 -> x0, waiting for transfers between devices: 39.6 us -> none  [body(): running = running + lax.psum(slab_sum, 'dp')]
    dot_general x8 -> x0, matrix products: 27.6 us -> none  [body(): jnp.einsum('jer,rp->jep', slab_block, probe_rows, preferred_element_type=...]
    scatter x1 -> x0, local copies, waits for them, and re-layouts: 15.5 us -> none  [body(): inverse = jnp.zeros((group_rows,), jnp.int32).at[local_row].set(jnp.arang...]
    convert_element_type x2 -> x0, other arithmetic: 13.6 us -> none  [the longest x1 13.5 us: body(): narrow = stored.astype(jnp.bfloat16)]
  transfers between devices with their start and end apart: 2 -> 0, of which waited for: 2 -> 0; matrix products, arithmetic and copies ran while one was open for 5% -> 0% of each run, Pallas kernels for 0% -> 0%
where the time goes in v1:
time: 475 us; the launch traced here: 473 us
  Pallas kernels  451 us (95%)
  local copies, waits for them, and re-layouts  20.3 us (4%)
    pallas_call x1, Pallas kernels, body(): pl.pallas_call(functools.partial(kernel, n_dp, n_mp), out_shape=(jax.Shap...  451 us
    unnamed x7, local copies, waits for them, and re-layouts  18.3 us

profile of v1, /device:TPU:0, one launch (start us, length us, event | category | flops | bytes accessed | tf_op | source)
XLA Modules:
  0.0 472.7 jit_solution(14803535339869363853)
XLA Ops:
  0.6 0.9 subtract_bitcast_fusion
  1.5 2.0 copy.7.local_row
  3.5 450.9 %shard_map.67 = (bf16[18,128,4096]{2,1,0:T(8,128)(2,1)}, f32[18,8,1024]{2,1,0:T(8,128)}, f32[18,1024]{1,0:T(8,128)}, bf16[9,32,128,256]{3,2,1,0:T(8,128)(2,1)}, bf16[9,32,128,256]{3,2,1,0:T(8,128)(2,1)}) custom-call(f32[512,18432]{1,0:T(8,128)} %stored.1, s32[4096,1]{1,0:T(8,128)} %copy.7.local_row, bf16[4096,1024]{1,0:T(8,128)(2,1)} %probe.1, ...), custom_call_target="tpu_custom_call" | custom-call | tf_op jit(solution)/shard_map/pallas_call | solution.py:194
  454.4 0.0 copy-start
  454.4 0.0 copy-start.1
  454.4 16.8 %copy.11 = bf16[18,128,4096]{2,1,0:T(8,128)(2,1)} copy(bf16[18,128,4096]{2,1,0:T(8,128)(2,1)} %get-tuple-element.12) | data formatting | bytes 37748736
  471.2 0.0 copy-done
  471.2 0.8 copy.12
  472.0 0.0 copy-done.1
  472.0 0.6 copy.13
Async XLA Ops:
  454.4 16.9 %copy-start = (f32[18,8,1024]{2,1,0:T(8,128)S(1)}, f32[18,8,1024]{2,1,0:T(8,128)}, u32[]{:S(2)}) copy-start(f32[18,8,1024]{2,1,0:T(8,128)} %get-tuple-element.13) | copy-start | bytes 1769476
  454.4 17.7 %copy-start.1 = (f32[18,1024]{1,0:T(8,128)S(1)}, f32[18,1024]{1,0:T(8,128)}, u32[]{:S(2)}) copy-start(f32[18,1024]{1,0:T(8,128)} %get-tuple-element.14) | copy-start | bytes 221188
